TPU v7x, 32 devices: a whole 2x2x4 slice. The times are simulated.
32 devices in a mesh: wide: 8 (over z, core), narrow: 4 (over y, x).
Axes of the slice: x: 2, y: 2, z: 4, core: 2. Of those that a mesh axis runs over, the one named last changes fastest.
Arguments:
- offsets: float32 [2, 8, 4, 8192], P(None, 'wide', 'narrow'), may hold values from -1 to 1
- strengths: float32 [2, 8, 4, 8192], P(None, 'wide', 'narrow'), may hold values from -1.2 to 1.2
- leaf_map: int32 [8, 4, 8192], P('wide', 'narrow'), may hold values from 0 to 1023
- shift_matrices: float32 [7, 4, 128, 128], replicated, may hold values from -0.25 to 0.25
- transfer_diagonal: float32 [5, 49, 128], replicated, may hold values from -1.25 to 1.25
Outputs:
- leaf_multipoles: float32 [256, 128, 128], P('wide', 'narrow')
- local_zero: float32 [8, 4, 128], P('wide', 'narrow')
- local_one: float32 [16, 8, 128], P('wide', 'narrow')
- local_two: float32 [32, 16, 128], P('wide', 'narrow')
- local_three: float32 [64, 32, 128], P('wide', 'narrow')
- coarse_local: float32 [4, 2, 128], replicated
- top_multipole: float32 [2, 1, 128], replicated
All inputs are finite; a program needn't handle non-finite values.
Results may differ from a plain program's by a relative error of at most 0.0003.
Values sent between devices are 32-bit elements; how exact they have to be, the bound alone decides.
A program may use at most 128 MiB of HBM per device.

v0:
```python
import math

import jax
import jax.numpy as jnp
from jax import lax
from jax.sharding import PartitionSpec as P

ORDER = 64
LOCAL = 5
COARSE = 2
LEAF_SIDE = 32


HIGHEST = lax.Precision.HIGHEST


def padded_2(cells, sides, width):
    for axis, dim in sides:
        count = lax.axis_size(axis)
        ends = count - 1
        head = lax.slice_in_dim(cells, 0, width, axis=dim)
        tail = lax.slice_in_dim(cells, cells.shape[dim] - width, cells.shape[dim], axis=dim)
        cells = jnp.concatenate(
            [
                lax.ppermute(tail, axis, [(i, (i + 1) % count) for i in range(ends)]),
                cells,
                lax.ppermute(head, axis, [((i + 1) % count, i) for i in range(ends)]),
            ],
            axis=dim,
        )
    return cells


def panel_terms(coords, charge):
    degree = jnp.arange(ORDER).astype(jnp.float32)
    cheb_first = jnp.cos(degree[None, :] * jnp.arccos(coords[0])[:, None])
    cheb_second = jnp.cos(degree[None, :] * jnp.arccos(coords[1])[:, None])
    real_part = charge[0][:, None] * cheb_first - charge[1][:, None] * cheb_second
    imag_part = charge[0][:, None] * cheb_second + charge[1][:, None] * cheb_first
    return jnp.concatenate([real_part, imag_part], axis=1)


def merge_children(children, operators):
    row_count, col_count, coeff_width = children.shape
    grouped = children.reshape(row_count // 2, 2, col_count // 2, 2, coeff_width)
    parent = jnp.zeros((row_count // 2 * (col_count // 2), coeff_width), jnp.float32)
    for row_bit in range(2):
        for col_bit in range(2):
            quarter = grouped[:, row_bit, :, col_bit, :].reshape(-1, coeff_width)
            parent = parent + jnp.dot(
                quarter,
                operators[2 * row_bit + col_bit],
                precision=HIGHEST,
                preferred_element_type=jnp.float32,
            )
    return parent.reshape(row_count // 2, col_count // 2, coeff_width)


def transfer(padded, diagonal, row_start, col_start, row_count, col_count):
    half_width = diagonal.shape[1] // 2
    row_parity = (row_start + jnp.arange(row_count, dtype=jnp.int32)) % 2
    col_parity = (col_start + jnp.arange(col_count, dtype=jnp.int32)) % 2
    summed = jnp.zeros((row_count, col_count, diagonal.shape[1]), jnp.float32)
    for shift_row in range(-3, 4):
        for shift_col in range(-3, 4):
            if max(abs(shift_row), abs(shift_col)) < 2:
                continue
            row_ok = ((shift_row >= -2 - row_parity) & (shift_row <= 3 - row_parity)).astype(
                jnp.float32
            )
            col_ok = ((shift_col >= -2 - col_parity) & (shift_col <= 3 - col_parity)).astype(
                jnp.float32
            )
            allowed = row_ok[:, None] * col_ok[None, :]
            source = padded[
                3 + shift_row : 3 + shift_row + row_count,
                3 + shift_col : 3 + shift_col + col_count,
                :,
            ]
            factor = diagonal[(shift_row + 3) * 7 + shift_col + 3]
            diag_real = factor[:half_width]
            diag_imag = factor[half_width:]
            src_real = source[..., :half_width]
            src_imag = source[..., half_width:]
            product = jnp.concatenate(
                [
                    diag_real * src_real - diag_imag * src_imag,
                    diag_real * src_imag + diag_imag * src_real,
                ],
                axis=-1,
            )
            summed = summed + allowed[:, :, None] * product
    return summed


def pad_grid(current):
    return jnp.pad(current, ((3, 3), (3, 3), (0, 0)))


def gather_top(pieces):
    along_row = (
        lax.all_gather(pieces[0], "narrow", axis=1, tiled=True),
        lax.all_gather(pieces[1], "narrow", axis=1, tiled=True),
    )
    result = (
        lax.all_gather(along_row[0], "wide", axis=0, tiled=True),
        lax.all_gather(along_row[1], "wide", axis=0, tiled=True),
    )
    return result


def own_region(whole, box_side, wide_at, narrow_at):
    coeff_width = whole.shape[2]
    return lax.dynamic_slice(
        pad_grid(whole),
        (wide_at * box_side, narrow_at * box_side, jnp.int32(0)),
        (box_side + 6, box_side + 6, coeff_width),
    )


def local(offsets, strengths, leaf_map, shift_matrices, transfer_diagonal):
    flat_coords = offsets.reshape(2, -1)
    flat_charge = strengths.reshape(2, -1)
    leaves = leaf_map.reshape(-1)
    panel_count = flat_coords.shape[1]
    block_size = math.gcd(panel_count, 2048)
    block_count = panel_count // block_size
    leaf_count = LEAF_SIDE * LEAF_SIDE
    leaf_ids = jnp.arange(leaf_count, dtype=jnp.int32)

    def add_block(totals, number):
        begin = number * block_size
        coords = lax.dynamic_slice_in_dim(flat_coords, begin, block_size, 1)
        charge = lax.dynamic_slice_in_dim(flat_charge, begin, block_size, 1)
        pieces = lax.dynamic_slice_in_dim(leaves, begin, block_size, 0)
        selector = (leaf_ids[:, None] == pieces[None, :]).astype(jnp.float32)
        return (
            totals
            + jnp.dot(
                selector,
                panel_terms(coords, charge),
                precision=HIGHEST,
                preferred_element_type=jnp.float32,
            ),
            None,
        )

    totals, _ = lax.scan(
        add_block,
        jnp.zeros((leaf_count, 2 * ORDER), jnp.float32),
        jnp.arange(block_count, dtype=jnp.int32),
    )
    leaf_grid = totals.reshape(LEAF_SIDE, LEAF_SIDE, 2 * ORDER)
    levels = {LOCAL: leaf_grid}
    for level in range(LOCAL - 1, -1, -1):
        levels[level] = merge_children(levels[level + 1], shift_matrices[COARSE + level])
    wide_at = lax.axis_index("wide")
    narrow_at = lax.axis_index("narrow")
    whole_zero, whole_one = gather_top((levels[0], levels[1]))
    regions = []
    for level in (2, 3):
        regions.append(padded_2(levels[level], (("wide", 0), ("narrow", 1)), 3))
    region_two = regions[0]
    region_three = regions[1]
    coarse_grid = merge_children(whole_zero, shift_matrices[1])
    top_grid = merge_children(coarse_grid, shift_matrices[0])
    coarse_local = transfer(
        pad_grid(coarse_grid),
        transfer_diagonal[0],
        0,
        0,
        coarse_grid.shape[0],
        coarse_grid.shape[1],
    )
    region_zero = own_region(whole_zero, 1, wide_at, narrow_at)
    local_zero = transfer(region_zero, transfer_diagonal[1], wide_at, narrow_at, 1, 1)
    region_one = own_region(whole_one, 2, wide_at, narrow_at)
    local_one = transfer(region_one, transfer_diagonal[2], wide_at * 2, narrow_at * 2, 2, 2)
    local_two = transfer(region_two, transfer_diagonal[3], wide_at * 4, narrow_at * 4, 4, 4)
    local_three = transfer(region_three, transfer_diagonal[4], wide_at * 8, narrow_at * 8, 8, 8)
    return (leaf_grid, local_zero, local_one, local_two, local_three, coarse_local, top_grid)


def solution(mesh):
    in_specs = (
        P(None, "wide", "narrow", None),
        P(None, "wide", "narrow", None),
        P("wide", "narrow", None),
        P(),
        P(),
    )
    out_specs = (
        P("wide", "narrow", None),
        P("wide", "narrow", None),
        P("wide", "narrow", None),
        P("wide", "narrow", None),
        P("wide", "narrow", None),
        P(),
        P(),
    )
    return jax.shard_map(local, mesh=mesh, in_specs=in_specs, out_specs=out_specs, check_vma=False)
```

profile of v0, /device:TPU:0, one launch (start us, length us, event | category | flops | bytes accessed | tf_op | source)
XLA Modules:
  0.0 153.9 jit_solution(874819929164682619)
XLA Ops:
  1.6 39.0 %while.11 = (s32[]{:T(128)}, f32[1024,128]{1,0:T(8,128)S(1)}, s32[4]{0:T(128)S(1)}, s32[8192]{0:T(1024)}, f32[2,8192]{1,0:T(2,128)S(1)}, /*index=5*/f32[2,8192]{...) while((s32[]{:T(128)}, f32[1024,128]{1,0:T(8,128)S(1)}, ...), condition=%wide.region_1.2_spmd.clone, body=%wide.region_0.1_spmd.clone.sunk | while | flops 3224907776 | bytes 3302097 | solution.py:148
  3.8 3.5 %multiply_subtract_fusion.174 = (f32[2048,64]{0,1:T(8,128)S(1)}, f32[2048,64]{0,1:T(8,128)S(1)}) fusion(f32[2048]{0:T(1024)S(1)} %sqrt_atan2_fusion.4, f32[2048]{0:T(1024)S(1)} %bitcast.904, f32[2048]{0:T(1024)S(1)} %sqrt_atan2_fusion.5, f32[64]{0:T(128)S(1)} %iota_convert_fusion.2, f32[2048]{0:T(1024)S(1)} %bitcast.903), kind=kLoop, calls=%fused_computation.9.clone.1 | loop fusion | flops 1048576 | bytes 1081600 | tf_op jit(solution)/shard_map/while/body/eval_jaxpr/sub | solution.py:38
  7.3 4.1 %fusion.313 = f32[1024,128]{1,0:T(8,128)S(1)} fusion(s32[2048]{0:T(1024)S(1)} %dynamic_slice.28, f32[2048,64]{0,1:T(8,128)S(1)} %get-tuple-element.1500, f32[2048,64]{0,1:T(8,128)S(1)} %get-tuple-element.1501, f32[1024,128]{1,0:T(8,128)S(1)} %get-tuple-element.1514, pred[]{:T(512)S(6)} %compare.106), kind=kOutput, calls=%fused_computation.4.clone.1 | convolution fusion | flops 3223846912 | bytes 2105345 | tf_op jit(solution)/shard_map/while/body/eval_jaxpr/dot_general | solution.py:139
  13.6 3.5 %multiply_subtract_fusion.174 = (f32[2048,64]{0,1:T(8,128)S(1)}, f32[2048,64]{0,1:T(8,128)S(1)}) fusion(f32[2048]{0:T(1024)S(1)} %sqrt_atan2_fusion.4, f32[2048]{0:T(1024)S(1)} %bitcast.904, f32[2048]{0:T(1024)S(1)} %sqrt_atan2_fusion.5, f32[64]{0:T(128)S(1)} %iota_convert_fusion.2, f32[2048]{0:T(1024)S(1)} %bitcast.903), kind=kLoop, calls=%fused_computation.9.clone.1 | loop fusion | flops 1048576 | bytes 1081600 | tf_op jit(solution)/shard_map/while/body/eval_jaxpr/sub | solution.py:38
  17.1 4.1 %fusion.313 = f32[1024,128]{1,0:T(8,128)S(1)} fusion(s32[2048]{0:T(1024)S(1)} %dynamic_slice.28, f32[2048,64]{0,1:T(8,128)S(1)} %get-tuple-element.1500, f32[2048,64]{0,1:T(8,128)S(1)} %get-tuple-element.1501, f32[1024,128]{1,0:T(8,128)S(1)} %get-tuple-element.1514, pred[]{:T(512)S(6)} %compare.106), kind=kOutput, calls=%fused_computation.4.clone.1 | convolution fusion | flops 3223846912 | bytes 2105345 | tf_op jit(solution)/shard_map/while/body/eval_jaxpr/dot_general | solution.py:139
  23.3 3.5 %multiply_subtract_fusion.174 = (f32[2048,64]{0,1:T(8,128)S(1)}, f32[2048,64]{0,1:T(8,128)S(1)}) fusion(f32[2048]{0:T(1024)S(1)} %sqrt_atan2_fusion.4, f32[2048]{0:T(1024)S(1)} %bitcast.904, f32[2048]{0:T(1024)S(1)} %sqrt_atan2_fusion.5, f32[64]{0:T(128)S(1)} %iota_convert_fusion.2, f32[2048]{0:T(1024)S(1)} %bitcast.903), kind=kLoop, calls=%fused_computation.9.clone.1 | loop fusion | flops 1048576 | bytes 1081600 | tf_op jit(solution)/shard_map/while/body/eval_jaxpr/sub | solution.py:38
  26.8 4.1 %fusion.313 = f32[1024,128]{1,0:T(8,128)S(1)} fusion(s32[2048]{0:T(1024)S(1)} %dynamic_slice.28, f32[2048,64]{0,1:T(8,128)S(1)} %get-tuple-element.1500, f32[2048,64]{0,1:T(8,128)S(1)} %get-tuple-element.1501, f32[1024,128]{1,0:T(8,128)S(1)} %get-tuple-element.1514, pred[]{:T(512)S(6)} %compare.106), kind=kOutput, calls=%fused_computation.4.clone.1 | convolution fusion | flops 3223846912 | bytes 2105345 | tf_op jit(solution)/shard_map/while/body/eval_jaxpr/dot_general | solution.py:139
  33.0 3.5 %multiply_subtract_fusion.174 = (f32[2048,64]{0,1:T(8,128)S(1)}, f32[2048,64]{0,1:T(8,128)S(1)}) fusion(f32[2048]{0:T(1024)S(1)} %sqrt_atan2_fusion.4, f32[2048]{0:T(1024)S(1)} %bitcast.904, f32[2048]{0:T(1024)S(1)} %sqrt_atan2_fusion.5, f32[64]{0:T(128)S(1)} %iota_convert_fusion.2, f32[2048]{0:T(1024)S(1)} %bitcast.903), kind=kLoop, calls=%fused_computation.9.clone.1 | loop fusion | flops 1048576 | bytes 1081600 | tf_op jit(solution)/shard_map/while/body/eval_jaxpr/sub | solution.py:38
  36.5 4.1 %fusion.313 = f32[1024,128]{1,0:T(8,128)S(1)} fusion(s32[2048]{0:T(1024)S(1)} %dynamic_slice.28, f32[2048,64]{0,1:T(8,128)S(1)} %get-tuple-element.1500, f32[2048,64]{0,1:T(8,128)S(1)} %get-tuple-element.1501, f32[1024,128]{1,0:T(8,128)S(1)} %get-tuple-element.1514, pred[]{:T(512)S(6)} %compare.106), kind=kOutput, calls=%fused_computation.4.clone.1 | convolution fusion | flops 3223846912 | bytes 2105345 | tf_op jit(solution)/shard_map/while/body/eval_jaxpr/dot_general | solution.py:139
  43.8 1.3 collective-permute-start.1
  45.1 3.0 %collective-permute-start = (f32[3,4,128]{2,1,0:T(4,128)S(1)}, f32[3,4,128]{2,1,0:T(4,128)S(1)}, u32[]{:S(2)}, u32[]{:S(2)}) collective-permute-start(f32[3,4,128]{2,1,0:T(4,128)S(1)} %slice.4962), channel_id=1, source_target_pairs={{0,4},{4,8},{8,12},{12,16},{16,20},{20,24},{24,28},{1,5},{5,9},{9,... | collective-permute-start | bytes 18440 | tf_op jit(solution)/shard_map/ppermute | solution.py:25
  48.1 1.3 collective-permute-start.5
  49.4 5.2 %collective-permute-start.4 = (f32[3,8,128]{2,1,0:T(8,128)S(1)}, f32[3,8,128]{2,1,0:T(8,128)S(1)}, u32[]{:S(2)}, u32[]{:S(2)}) collective-permute-start(f32[3,8,128]{2,1,0:T(8,128)S(1)} %get-tuple-element.1131), channel_id=1, source_target_pairs={{0,4},{4,8},{8,12},{12,16},{16,20},{20,24},{24,28},{1,5},{5,9},{9,... | collective-permute-start | bytes 36872 | tf_op jit(solution)/shard_map/ppermute | solution.py:25
  56.0 8.0 %all-gather.1 = f32[4,1,128]{2,1,0:T(1,128)S(1)} all-gather(f32[1,1,128]{2,1,0:T(1,128)S(1)} %fusion.10), channel_id=2, replica_groups=mesh['wide'=8,'narrow'=4] {'narrow'}, dimensions={0}, use_global_device_ids=true | all-gather | bytes 2560 | tf_op jit(solution)/shard_map/all_gather | solution.py:102
  64.0 13.2 %all_gather.13 = f32[8,4,128]{2,1,0:T(4,128)S(1)} all-gather(f32[1,4,128]{2,1,0:T(4,128)S(1)} %bitcast.941), channel_id=1, replica_groups=mesh['wide'=8,'narrow'=4] {'wide'}, dimensions={0}, use_global_device_ids=true | all-gather | bytes 18432 | tf_op jit(solution)/shard_map/all_gather | solution.py:106
  97.8 8.1 %all_gather.14 = f32[2,8,128]{2,0,1:T(2,128)S(1)} all-gather(f32[2,2,128]{2,0,1:T(2,128)S(1)} %copy.28), channel_id=1, replica_groups=mesh['wide'=8,'narrow'=4] {'narrow'}, dimensions={1}, use_global_device_ids=true | all-gather | bytes 10240 | tf_op jit(solution)/shard_map/all_gather | solution.py:103
  105.9 14.0 %all_gather.15 = f32[16,8,128]{2,1,0:T(8,128)S(1)} all-gather(f32[2,8,128]{2,1,0:T(8,128)S(1)} %copy.29), channel_id=1, replica_groups=mesh['wide'=8,'narrow'=4] {'wide'}, dimensions={0}, use_global_device_ids=true | all-gather | bytes 73728 | tf_op jit(solution)/shard_map/all_gather | solution.py:107
  135.8 1.3 collective-permute-start.3
  137.1 4.5 %collective-permute-start.2 = (f32[10,3,128]{2,1,0:T(4,128)S(1)}, f32[10,3,128]{2,1,0:T(4,128)S(1)}, u32[]{:S(2)}, u32[]{:S(2)}) collective-permute-start(f32[10,3,128]{2,1,0:T(4,128)S(1)} %get-tuple-element.1140), channel_id=1, source_target_pairs={{0,1},{1,2},{2,3},{4,5},{5,6},{6,7},{8,9},{9,10},{10,11},{12,13},{... | collective-permute-start | bytes 46088 | tf_op jit(solution)/shard_map/ppermute | solution.py:25
  141.9 3.3 %collective-permute-start.6 = (f32[14,3,128]{2,1,0:T(4,128)S(1)}, f32[14,3,128]{2,1,0:T(4,128)S(1)}, u32[]{:S(2)}, u32[]{:S(2)}) collective-permute-start(f32[14,3,128]{2,1,0:T(4,128)S(1)} %get-tuple-element.997), channel_id=1, source_target_pairs={{0,1},{1,2},{2,3},{4,5},{5,6},{6,7},{8,9},{9,10},{10,11},{12,13},{... | collective-permute-start | bytes 64520 | tf_op jit(solution)/shard_map/ppermute | solution.py:25
  145.2 1.3 collective-permute-start.7
  147.9 1.3 fusion.164
  149.1 1.8 %collective-permute-done.7 = f32[14,3,128]{2,1,0:T(4,128)S(1)} collective-permute-done((f32[14,3,128]{2,1,0:T(4,128)S(1)}, f32[14,3,128]{2,1,0:T(4,128)S(1)}, u32[]{:S(2)}, u32[]{:S(2)}) %collective-permute-start.7) | collective-permute-done | bytes 21536 | tf_op jit(solution)/shard_map/ppermute | solution.py:27
  152.3 1.6 %fusion.119 = f32[8,8,128]{2,1,0:T(8,128)} fusion(f32[8,8,64]{2,1,0:T(8,128)S(1)} %get-tuple-element.905, f32[8,8,64]{2,1,0:T(8,128)S(1)} %get-tuple-element.906, f32[8,8,64]{2,1,0:T(8,128)S(1)} %get-tuple-element.879, f32[8,8,64]{2,1,0:T(8,128)S(1)} %get-tuple-element.880, f32[8,8,64]{2,1,0:T(8,128)S(1)} %get-tuple-element.877, ...), kind=kLoop, calls=%fused_computation.381 | loop fusion | flops 974848 | bytes 1353728 | tf_op jit(solution)/shard_map/add | solution.py:92
  (334 shorter events, 49.6 us)
Async XLA Ops:
  1.6 39.4 %copy-start = (f32[7,4,128,128]{3,2,1,0:T(8,128)S(1)}, f32[7,4,128,128]{3,2,1,0:T(8,128)}, u32[]{:S(2)}) copy-start(f32[7,4,128,128]{3,2,1,0:T(8,128)} %param.10) | copy-start | bytes 5505028
  41.3 35.9 %copy-start.2 = (f32[5,49,128]{2,1,0:T(8,128)S(1)}, f32[5,49,128]{2,1,0:T(8,128)}, u32[]{:S(2)}) copy-start(f32[5,49,128]{2,1,0:T(8,128)} %param.11) | copy-start | bytes 376324
  43.8 92.0 %collective-permute-start.1 = (f32[3,4,128]{2,1,0:T(4,128)S(1)}, f32[3,4,128]{2,1,0:T(4,128)S(1)}, u32[]{:S(2)}, u32[]{:S(2)}) collective-permute-start(f32[3,4,128]{2,1,0:T(4,128)S(1)} %slice.4964), channel_id=1, source_target_pairs={{4,0},{8,4},{12,8},{16,12},{20,16},{24,20},{28,24},{5,1},{9,5},{13... | collective-permute-start | bytes 18440 | tf_op jit(solution)/shard_map/ppermute | solution.py:27
  45.1 90.7 %collective-permute-start = (f32[3,4,128]{2,1,0:T(4,128)S(1)}, f32[3,4,128]{2,1,0:T(4,128)S(1)}, u32[]{:S(2)}, u32[]{:S(2)}) collective-permute-start(f32[3,4,128]{2,1,0:T(4,128)S(1)} %slice.4962), channel_id=1, source_target_pairs={{0,4},{4,8},{8,12},{12,16},{16,20},{20,24},{24,28},{1,5},{5,9},{9,... | collective-permute-start | bytes 18440 | tf_op jit(solution)/shard_map/ppermute | solution.py:25
  48.1 93.7 %collective-permute-start.5 = (f32[3,8,128]{2,1,0:T(8,128)S(1)}, f32[3,8,128]{2,1,0:T(8,128)S(1)}, u32[]{:S(2)}, u32[]{:S(2)}) collective-permute-start(f32[3,8,128]{2,1,0:T(8,128)S(1)} %get-tuple-element.1132), channel_id=1, source_target_pairs={{4,0},{8,4},{12,8},{16,12},{20,16},{24,20},{28,24},{5,1},{9,5},{13... | collective-permute-start | bytes 36872 | tf_op jit(solution)/shard_map/ppermute | solution.py:27
  49.4 92.4 %collective-permute-start.4 = (f32[3,8,128]{2,1,0:T(8,128)S(1)}, f32[3,8,128]{2,1,0:T(8,128)S(1)}, u32[]{:S(2)}, u32[]{:S(2)}) collective-permute-start(f32[3,8,128]{2,1,0:T(8,128)S(1)} %get-tuple-element.1131), channel_id=1, source_target_pairs={{0,4},{4,8},{8,12},{12,16},{16,20},{20,24},{24,28},{1,5},{5,9},{9,... | collective-permute-start | bytes 36872 | tf_op jit(solution)/shard_map/ppermute | solution.py:25
  96.8 35.7 %copy-start.13 = (f32[2]{0:T(128)S(1)}, f32[2]{0:T(128)}, u32[]{:S(2)}) copy-start(f32[2]{0:T(128)} %get-tuple-element.1421) | copy-start | bytes 28
  96.9 35.7 %copy-start.14 = (f32[2]{0:T(128)S(1)}, f32[2]{0:T(128)}, u32[]{:S(2)}) copy-start(f32[2]{0:T(128)} %get-tuple-element.1422) | copy-start | bytes 28
  97.0 35.8 %copy-start.25 = (f32[4]{0:T(128)S(1)}, f32[4]{0:T(128)}, u32[]{:S(2)}) copy-start(f32[4]{0:T(128)} %get-tuple-element.1409) | copy-start | bytes 52
  97.0 35.8 %copy-start.26 = (f32[4]{0:T(128)S(1)}, f32[4]{0:T(128)}, u32[]{:S(2)}) copy-start(f32[4]{0:T(128)} %get-tuple-element.1410) | copy-start | bytes 52
  97.0 35.8 %copy-start.27 = (f32[4]{0:T(128)S(1)}, f32[4]{0:T(128)}, u32[]{:S(2)}) copy-start(f32[4]{0:T(128)} %and_convert_fusion.41) | copy-start | bytes 52
  97.0 35.8 %copy-start.28 = (f32[4]{0:T(128)S(1)}, f32[4]{0:T(128)}, u32[]{:S(2)}) copy-start(f32[4]{0:T(128)} %get-tuple-element.1407) | copy-start | bytes 52
  97.0 35.8 %copy-start.29 = (f32[4]{0:T(128)S(1)}, f32[4]{0:T(128)}, u32[]{:S(2)}) copy-start(f32[4]{0:T(128)} %get-tuple-element.1408) | copy-start | bytes 52
  97.0 35.8 %copy-start.30 = (f32[4]{0:T(128)S(1)}, f32[4]{0:T(128)}, u32[]{:S(2)}) copy-start(f32[4]{0:T(128)} %get-tuple-element.1399) | copy-start | bytes 52
  97.0 35.8 %copy-start.31 = (f32[4]{0:T(128)S(1)}, f32[4]{0:T(128)}, u32[]{:S(2)}) copy-start(f32[4]{0:T(128)} %get-tuple-element.1400) | copy-start | bytes 52
  97.0 35.8 %copy-start.32 = (f32[4]{0:T(128)S(1)}, f32[4]{0:T(128)}, u32[]{:S(2)}) copy-start(f32[4]{0:T(128)} %get-tuple-element.1384) | copy-start | bytes 52
  97.0 35.8 %copy-start.33 = (f32[4]{0:T(128)S(1)}, f32[4]{0:T(128)}, u32[]{:S(2)}) copy-start(f32[4]{0:T(128)} %get-tuple-element.1405) | copy-start | bytes 52
  97.1 35.8 %copy-start.34 = (f32[4]{0:T(128)S(1)}, f32[4]{0:T(128)}, u32[]{:S(2)}) copy-start(f32[4]{0:T(128)} %get-tuple-element.1406) | copy-start | bytes 52
  97.1 35.8 %copy-start.35 = (f32[4]{0:T(128)S(1)}, f32[4]{0:T(128)}, u32[]{:S(2)}) copy-start(f32[4]{0:T(128)} %get-tuple-element.1401) | copy-start | bytes 52
  97.1 35.8 %copy-start.36 = (f32[4]{0:T(128)S(1)}, f32[4]{0:T(128)}, u32[]{:S(2)}) copy-start(f32[4]{0:T(128)} %get-tuple-element.1402) | copy-start | bytes 52
  135.8 11.0 %collective-permute-start.3 = (f32[10,3,128]{2,1,0:T(4,128)S(1)}, f32[10,3,128]{2,1,0:T(4,128)S(1)}, u32[]{:S(2)}, u32[]{:S(2)}) collective-permute-start(f32[10,3,128]{2,1,0:T(4,128)S(1)} %get-tuple-element.1139), channel_id=1, source_target_pairs={{1,0},{2,1},{3,2},{5,4},{6,5},{7,6},{9,8},{10,9},{11,10},{13,12},{... | collective-permute-start | bytes 46088 | tf_op jit(solution)/shard_map/ppermute | solution.py:27
  137.1 9.7 %collective-permute-start.2 = (f32[10,3,128]{2,1,0:T(4,128)S(1)}, f32[10,3,128]{2,1,0:T(4,128)S(1)}, u32[]{:S(2)}, u32[]{:S(2)}) collective-permute-start(f32[10,3,128]{2,1,0:T(4,128)S(1)} %get-tuple-element.1140), channel_id=1, source_target_pairs={{0,1},{1,2},{2,3},{4,5},{5,6},{6,7},{8,9},{9,10},{10,11},{12,13},{... | collective-permute-start | bytes 46088 | tf_op jit(solution)/shard_map/ppermute | solution.py:25
  141.9 7.3 %collective-permute-start.6 = (f32[14,3,128]{2,1,0:T(4,128)S(1)}, f32[14,3,128]{2,1,0:T(4,128)S(1)}, u32[]{:S(2)}, u32[]{:S(2)}) collective-permute-start(f32[14,3,128]{2,1,0:T(4,128)S(1)} %get-tuple-element.997), channel_id=1, source_target_pairs={{0,1},{1,2},{2,3},{4,5},{5,6},{6,7},{8,9},{9,10},{10,11},{12,13},{... | collective-permute-start | bytes 64520 | tf_op jit(solution)/shard_map/ppermute | solution.py:25
  145.2 5.8 %collective-permute-start.7 = (f32[14,3,128]{2,1,0:T(4,128)S(1)}, f32[14,3,128]{2,1,0:T(4,128)S(1)}, u32[]{:S(2)}, u32[]{:S(2)}) collective-permute-start(f32[14,3,128]{2,1,0:T(4,128)S(1)} %get-tuple-element.998), channel_id=1, source_target_pairs={{1,0},{2,1},{3,2},{5,4},{6,5},{7,6},{9,8},{10,9},{11,10},{13,12},{... | collective-permute-start | bytes 64520 | tf_op jit(solution)/shard_map/ppermute | solution.py:27
  (21 other events, 627.4 us)
where the time goes:
time: 155 us; the launch traced here: 154 us
  other arithmetic  52 us (34%)
  blocking collectives  43.2 us (28%)
  matrix products  21.9 us (14%)
  starting transfers between devices  21.3 us (14%)
  local copies, waits for them, and re-layouts  8.75 us (6%)
  loops' own time  2.86 us (2%)
  between operations  2.02 us (1%)
  waiting for transfers between devices  1.84 us (1%)
    dot_general x4, matrix products, add_block(): jnp.dot(selector, panel_terms(coords, charge), precision=HIGHEST, preferr...  16.2 us
    ppermute x4, starting transfers between devices, padded_2(): lax.ppermute(tail, axis, [(i, (i + 1) % count) for i in range(ends)])  16.1 us
    all_gather x1, blocking collectives, gather_top(): lax.all_gather(along_row[1], 'wide', axis=0, tiled=True)  14 us
    sub x4, other arithmetic, panel_terms(): charge[0][:, None] * cheb_first - charge[1][:, None] * cheb_second  13.9 us
    sub x63, other arithmetic, transfer(): diag_real * src_real - diag_imag * src_imag  13.4 us
    all_gather x1, blocking collectives, gather_top(): lax.all_gather(along_row[0], 'wide', axis=0, tiled=True)  13.2 us
    add x55, other arithmetic, transfer(): diag_real * src_imag + diag_imag * src_real  8.85 us
    all_gather x1, blocking collectives, gather_top(): lax.all_gather(pieces[1], 'narrow', axis=1, tiled=True)  8.07 us
  transfers between devices with their start and end apart: 8, of which 1 were waited for; matrix products, arithmetic and copies ran while one was open for 26% of the time, Pallas kernels for 0%

commit v1 on v0

v1 whole, which is shorter than its diff:
```python
import functools

import jax
import jax.numpy as jnp
from jax import lax
from jax.experimental import pallas as pl
from jax.experimental.pallas import tpu as pltpu
from jax.sharding import PartitionSpec as P

F32 = jnp.float32
BF16 = jnp.bfloat16
MESH = pl.DeviceIdType.MESH
COARSE = 2
SIDE = 32
REACH = 3


def split(x):
    hi = x.astype(BF16)
    return hi, (x - hi.astype(F32)).astype(BF16)


def dot(a, b):
    return jnp.dot(a, b, preferred_element_type=F32)


def merge(parts, weight):
    width = parts[0].shape[1]
    lhs = jnp.concatenate(parts, axis=1)
    hi, lo = split(lhs)
    w_hi, w_lo = split(weight)
    both = dot(hi, jnp.concatenate([w_hi, w_lo], axis=1))
    return both[:, :width] + (both[:, width:] + dot(lo, w_hi))


def cheb_start(a):
    k = lax.broadcasted_iota(jnp.int32, a.shape, 0)
    t = [jnp.ones_like(a), a]
    twice = a + a
    for _ in range(7):
        t.append(twice * t[-1] - t[-2])
    cur, prev = t[0], t[8]
    for n in range(1, 8):
        cur = jnp.where(k == n, t[n], cur)
        prev = jnp.where(k == n, t[8 - n], prev)
    return t[8] + t[8], prev, cur


def panel_kernel(order, chunk, off_ref, str_ref, map_ref, shift_ref, leaf_ref, l3_ref, l2_ref, l01_ref, acc_ref):
    panels = off_ref.shape[-1]
    leaves = SIDE * SIDE
    acc_ref[...] = jnp.zeros_like(acc_ref)

    def body(i, carry):
        at = pl.ds(pl.multiple_of(i * chunk, chunk), chunk)
        wide8 = lambda ref, n: jnp.broadcast_to(ref[n, 0, :, at], (8, chunk))
        a, b = wide8(off_ref, 0), wide8(off_ref, 1)
        qr, qi = wide8(str_ref, 0), wide8(str_ref, 1)
        ma, pa, ca = cheb_start(a)
        mb, pb, cb = cheb_start(b)
        real, imag = [], []
        for j in range(order // 8):
            real.append(qr * ca - qi * cb)
            imag.append(qr * cb + qi * ca)
            if j + 1 < order // 8:
                ca, pa = ma * ca - pa, ca
                cb, pb = mb * cb - pb, cb
        hi, lo = split(jnp.concatenate(real + imag, axis=0))
        terms = jnp.concatenate([hi, lo], axis=0)
        leaf = jnp.broadcast_to(map_ref[0, :, at], (SIDE, chunk))
        row = (leaf // SIDE).astype(F32).astype(BF16)
        col = leaf % SIDE
        one = (col == lax.broadcasted_iota(jnp.int32, (SIDE, chunk), 0)).astype(F32).astype(BF16)
        zero = jnp.zeros_like(one)
        sel = jnp.concatenate([jnp.where(row == r, one, zero) for r in range(SIDE)], axis=0)
        acc_ref[...] += lax.dot_general(sel, terms, (((1,), (1,)), ((), ())), preferred_element_type=F32)
        return carry

    lax.fori_loop(0, panels // chunk, body, 0)
    width = 2 * order
    leaf_ref[...] = acc_ref[:, :width] + acc_ref[:, width:]

    def weight(level):
        return shift_ref[COARSE + level].reshape(4 * width, width)

    parts = []
    for r0 in range(2):
        for c0 in range(2):
            rows = []
            for r1 in range(2):
                for c1 in range(2):
                    for top in range(8):
                        start = (4 * top + 2 * r1 + r0) * SIDE + 2 * c1 + c0
                        rows.append(leaf_ref[pl.ds(start, 8, stride=4), :])
            parts.append(jnp.concatenate(rows, axis=0))
    level4 = merge(parts, weight(4))
    level3 = merge([level4[64 * q : 64 * q + 64] for q in range(4)], weight(3))
    l3_ref[...] = level3
    parts = []
    for rb in range(2):
        for cb in range(2):
            parts.append(jnp.concatenate([l3_ref[pl.ds((2 * r + rb) * 8 + cb, 4, stride=2), :] for r in range(4)], axis=0))
    l2_ref[...] = merge(parts, weight(2))
    parts = []
    for rb in range(2):
        for cb in range(2):
            parts.append(jnp.concatenate([l2_ref[pl.ds((2 * r + rb) * 4 + cb, 2, stride=2), :] for r in range(2)], axis=0))
    level1 = merge(parts, weight(1))
    level0 = merge([level1[q : q + 1] for q in range(4)], weight(0))
    l01_ref[...] = jnp.concatenate([level0, level1, jnp.zeros((3, width), F32)], axis=0)


NEAR = [(dr, dc) for dr in range(-3, 4) for dc in range(-3, 4) if max(abs(dr), abs(dc)) >= 2]
AROUND = [(dw, dv) for dw in (-1, 0, 1) for dv in (-1, 0, 1) if (dw, dv) != (0, 0)]


def allowed(d, parity):
    return -2 - parity <= d <= 3 - parity


def exchange_kernel(
    rows, cols,
    l3_ref, l2_ref, l01_ref, shift_ref, diag_ref,
    zero_out, one_out, two_out, three_out, coarse_out, top_out,
    reg3, slots2, big, pad2, sh3, sh2, xr, xi, lhs, grid1,
    send_all, recv_all, send_near, recv_near,
):
    w, v = lax.axis_index("wide"), lax.axis_index("narrow")
    count = rows * cols
    me = w * cols + v
    width = l01_ref.shape[-1]
    half = width // 2

    barrier = pltpu.get_barrier_semaphore()

    def greet(i, carry):
        t = lax.rem(me + i, count)
        pl.semaphore_signal(barrier, inc=1, device_id=(t // cols, lax.rem(t, cols)), device_id_type=MESH)
        return carry

    lax.fori_loop(1, count, greet, 0)
    pl.semaphore_wait(barrier, count - 1)

    row_of = {-1: 0, 0: 0, 1: 5}
    row_to = {-1: 11, 0: 3, 1: 0}
    row_n = {-1: 3, 0: 8, 1: 3}
    col_to = {-1: 16, 0: 8, 1: 0}

    def inside(dw, dv):
        ok = jnp.bool_(True)
        if dw < 0:
            ok = w > 0
        if dw > 0:
            ok = w < rows - 1
        if dv < 0:
            ok = ok & (v > 0)
        if dv > 0:
            ok = ok & (v < cols - 1)
        return ok

    def near_copies(dw, dv):
        slot = (1 - dw) * 3 + (1 - dv)
        target = (w + dw, v + dv)
        three = pltpu.make_async_remote_copy(
            src_ref=l3_ref.at[pl.ds(row_of[dw], row_n[dw])],
            dst_ref=reg3.at[pl.ds(row_to[dw], row_n[dw]), pl.ds(col_to[dv], 8)],
            send_sem=send_near.at[0, slot], recv_sem=recv_near.at[0, slot],
            device_id=target, device_id_type=MESH)
        two = pltpu.make_async_remote_copy(
            src_ref=l2_ref, dst_ref=slots2.at[slot],
            send_sem=send_near.at[1, slot], recv_sem=recv_near.at[1, slot],
            device_id=target, device_id_type=MESH)
        return three, two

    def all_copy(t, source):
        sw, sv = source // cols, lax.rem(source, cols)
        return pltpu.make_async_remote_copy(
            src_ref=l01_ref, dst_ref=big.at[3 + sw, 3 + sv],
            send_sem=send_all.at[t], recv_sem=recv_all.at[source],
            device_id=(t // cols, lax.rem(t, cols)), device_id_type=MESH)

    def send(i, carry):
        all_copy(lax.rem(me + i, count), me).start()
        return carry

    lax.fori_loop(1, count, send, 0)
    for dw, dv in AROUND:
        @pl.when(inside(dw, dv))
        def _():
            for copy in near_copies(dw, dv):
                copy.start()

    tile = jnp.zeros((8, width), F32)
    for dw, dv in AROUND:
        @pl.when(jnp.logical_not(inside(dw, dv)))
        def _():
            for r in range(row_n[-dw]):
                reg3[row_to[-dw] + r, pl.ds(col_to[-dv], 8)] = tile
            slot = (1 + dw) * 3 + (1 + dv)
            slots2[slot] = jnp.zeros((16, width), F32)
    for r in range(rows + 6):
        for c in range(cols + 6):
            if not (3 <= r < rows + 3 and 3 <= c < cols + 3):
                big[r, c] = tile
    big[3 + w, 3 + v] = l01_ref[...]
    for r in range(8):
        reg3[3 + r, pl.ds(8, 8)] = l3_ref[r]
    slots2[4] = l2_ref[...]
    for r in range(10):
        pad2[r, pl.ds(8, 8)] = tile

    lane = lax.broadcasted_iota(jnp.int32, (diag_ref.shape[1], width), 1) < half
    for s in range(diag_ref.shape[0]):
        d = diag_ref[s]
        turned = pltpu.roll(d, half, 1)
        xr[s] = jnp.where(lane, d, turned)
        xi[s] = jnp.where(lane, turned, d)
    sign = jnp.where(lax.broadcasted_iota(jnp.int32, (1, width), 1) < half, -1.0, 1.0).astype(F32)
    c_id = lax.broadcasted_iota(jnp.int32, (8, width), 0)
    odd = lax.rem(c_id, 2) == 1

    def col_mask(dc, slab):
        if dc == -3:
            return jnp.where(odd, slab, 0.0)
        if dc == 3:
            return jnp.where(odd, 0.0, slab)
        return slab

    def factor(s, dr, dc):
        at = pl.ds(7 * (dr + 3) + dc + 3, 1)
        return xr[s, at, :], xi[s, at, :]

    def finish(acc_r, acc_i):
        return acc_r + sign * pltpu.roll(acc_i, half, 1)

    def near_level(s, n, shifted, out):
        acc_r = [jnp.zeros((8, width), F32) for _ in range(n)]
        acc_i = [jnp.zeros((8, width), F32) for _ in range(n)]
        for dr, dc in NEAR:
            f_r, f_i = factor(s, dr, dc)
            for r in range(n):
                if allowed(dr, r % 2):
                    src = shifted[dc + 3, 3 + r + dr]
                    acc_r[r] = acc_r[r] + f_r * src
                    acc_i[r] = acc_i[r] + f_i * src
        for r in range(n):
            out[r] = finish(acc_r[r], acc_i[r])[: out.shape[1]]

    for dw, dv in AROUND:
        @pl.when(inside(dw, dv))
        def _():
            for copy in near_copies(-dw, -dv):
                copy.wait_recv()

    for dc in range(-3, 4):
        for r in range(14):
            sh3[dc + 3, r] = col_mask(dc, reg3[r, pl.ds(8 + dc, 8)])
    near_level(4, 8, sh3, three_out)

    for dw in (-1, 0, 1):
        for dv in (-1, 0, 1):
            slot = (1 + dw) * 3 + (1 + dv)
            for r in range(4):
                at = 3 + 4 * dw + r
                if 0 <= at < 10:
                    pad2[at, pl.ds(4 + 4 * dv, 4)] = slots2[slot, pl.ds(4 * r, 4)]
    for dc in range(-3, 4):
        for r in range(10):
            sh2[dc + 3, r] = col_mask(dc, pad2[r, pl.ds(4 + dc, 8)])
    near_level(3, 4, sh2, two_out)

    def arrive(i, carry):
        s = lax.rem(me + i, count)
        all_copy(s, s).wait_recv()
        return carry

    lax.fori_loop(1, count, arrive, 0)

    half_r, half_c = rows // 2, cols // 2
    for r in range(rows):
        for c in range(cols):
            q = 2 * (r % 2) + c % 2
            lhs[pl.ds((r // 2) * half_c + c // 2, 1), pl.ds(q * width, width)] = big[3 + r, 3 + c, pl.ds(0, 1)]
    boxes = half_r * half_c

    def weight(t):
        return shift_ref[t].reshape(4 * width, width)

    coarse = merge([lhs[:boxes, pl.ds(q * width, width)] for q in range(4)], weight(1))
    grid1[:boxes] = coarse
    quarter_c = half_c // 2
    for r in range(half_r):
        for c in range(half_c):
            q = 2 * (r % 2) + c % 2
            lhs[pl.ds((r // 2) * quarter_c + c // 2, 1), pl.ds(q * width, width)] = grid1[pl.ds(r * half_c + c, 1)]
    tops = (half_r // 2) * quarter_c
    top = merge([lhs[:tops, pl.ds(q * width, width)] for q in range(4)], weight(0))
    for r in range(half_r // 2):
        top_out[r] = top[r * quarter_c : (r + 1) * quarter_c]

    for tr in range(2):
        line = []
        for tc in range(2):
            acc_r = jnp.zeros((1, width), F32)
            acc_i = jnp.zeros((1, width), F32)
            for dr, dc in NEAR:
                if allowed(dr, tr) and allowed(dc, tc):
                    f_r, f_i = factor(2, dr, dc)
                    sr, sc = tr + dr, tc + dc
                    src = big[3 + w + sr // 2, 3 + v + sc // 2, pl.ds(1 + 2 * (sr % 2) + sc % 2, 1)]
                    acc_r = acc_r + f_r * src
                    acc_i = acc_i + f_i * src
            line.append(finish(acc_r, acc_i))
        one_out[tr] = jnp.concatenate(line, axis=0)

    odd_w, odd_v = lax.rem(w, 2), lax.rem(v, 2)
    keep = {
        ("r", -3): odd_w.astype(F32), ("r", 3): (1 - odd_w).astype(F32),
        ("c", -3): odd_v.astype(F32), ("c", 3): (1 - odd_v).astype(F32),
    }
    acc_r = jnp.zeros((1, width), F32)
    acc_i = jnp.zeros((1, width), F32)
    for dr, dc in NEAR:
        f_r, f_i = factor(1, dr, dc)
        src = big[3 + w + dr, 3 + v + dc, pl.ds(0, 1)]
        if abs(dr) == 3:
            src = src * keep["r", dr]
        if abs(dc) == 3:
            src = src * keep["c", dc]
        acc_r = acc_r + f_r * src
        acc_i = acc_i + f_i * src
    zero_out[0] = finish(acc_r, acc_i)

    for r in range(half_r):
        line = []
        for c in range(half_c):
            acc_r = jnp.zeros((1, width), F32)
            acc_i = jnp.zeros((1, width), F32)
            for dr, dc in NEAR:
                if allowed(dr, r % 2) and allowed(dc, c % 2) and 0 <= r + dr < half_r and 0 <= c + dc < half_c:
                    f_r, f_i = factor(0, dr, dc)
                    src = grid1[pl.ds((r + dr) * half_c + c + dc, 1)]
                    acc_r = acc_r + f_r * src
                    acc_i = acc_i + f_i * src
            line.append(finish(acc_r, acc_i))
        coarse_out[r] = jnp.concatenate(line, axis=0)

    for dw, dv in AROUND:
        @pl.when(inside(dw, dv))
        def _():
            for copy in near_copies(dw, dv):
                copy.wait_send()

    def left(i, carry):
        all_copy(lax.rem(me + i, count), me).wait_send()
        return carry

    lax.fori_loop(1, count, left, 0)


def local(mesh_shape, offsets, strengths, leaf_map, shift_matrices, transfer_diagonal):
    rows, cols = mesh_shape
    width = shift_matrices.shape[-1]
    order = width // 2
    levels = transfer_diagonal.shape[0]
    vmem = pl.BlockSpec(memory_space=pltpu.VMEM)
    shape = lambda *dims: jax.ShapeDtypeStruct(dims, F32)
    leaf, l3, l2, l01 = pl.pallas_call(
        functools.partial(panel_kernel, order, 512),
        out_shape=(shape(SIDE * SIDE, width), shape(64, width), shape(16, width), shape(8, width)),
        in_specs=[vmem] * 4,
        out_specs=(vmem,) * 4,
        scratch_shapes=[pltpu.VMEM((SIDE * SIDE, 2 * width), F32)],
        name="panels",
    )(offsets, strengths, leaf_map, shift_matrices)
    boxes = (rows // 2) * (cols // 2)
    pad8 = -(-boxes // 8) * 8
    outs = pl.pallas_call(
        functools.partial(exchange_kernel, rows, cols),
        out_shape=(
            shape(1, 1, width), shape(2, 2, width), shape(4, 4, width), shape(8, 8, width),
            shape(rows // 2, cols // 2, width), shape(rows // 4, cols // 4, width),
        ),
        grid=(1,),
        in_specs=[vmem, vmem, vmem, pl.BlockSpec((2, 4, width, width), lambda i: (0, 0, 0, 0)), vmem],
        out_specs=(vmem,) * 6,
        scratch_shapes=[
            pltpu.VMEM((14, 24, width), F32),
            pltpu.VMEM((9, 16, width), F32),
            pltpu.VMEM((rows + 6, cols + 6, 8, width), F32),
            pltpu.VMEM((10, 16, width), F32),
            pltpu.VMEM((7, 14, 8, width), F32),
            pltpu.VMEM((7, 10, 8, width), F32),
            pltpu.VMEM((levels, 49, width), F32),
            pltpu.VMEM((levels, 49, width), F32),
            pltpu.VMEM((pad8, 4 * width), F32),
            pltpu.VMEM((pad8, width), F32),
            pltpu.SemaphoreType.DMA((rows * cols,)),
            pltpu.SemaphoreType.DMA((rows * cols,)),
            pltpu.SemaphoreType.DMA((2, 9)),
            pltpu.SemaphoreType.DMA((2, 9)),
        ],
        compiler_params=pltpu.CompilerParams(collective_id=0, has_side_effects=True),
        name="exchange",
    )(l3.reshape(8, 8, width), l2, l01, shift_matrices, transfer_diagonal)
    return (leaf.reshape(SIDE, SIDE, width),) + tuple(outs)


def solution(mesh):
    split_2 = P("wide", "narrow", None)
    in_specs = (P(None, "wide", "narrow", None), P(None, "wide", "narrow", None), split_2, P(), P())
    out_specs = (split_2,) * 5 + (P(), P())
    body = functools.partial(local, (mesh.shape["wide"], mesh.shape["narrow"]))
    return jax.shard_map(body, mesh=mesh, in_specs=in_specs, out_specs=out_specs, check_vma=False)
```

time: 155 us -> 36.5 us (0.24)
  the two profiles are of different devices: /device:TPU:0 before, /device:TPU:1 now
where the time goes in v1:
time: 36.5 us; the launch traced here: 36.2 us
  Pallas kernels  28 us (77%)
  local copies, waits for them, and re-layouts  7.55 us (21%)
  between operations  0.64 us (2%)
    pallas_call x1, Pallas kernels, local(): pl.pallas_call(functools.partial(exchange_kernel, rows, cols), out_shape=...  16 us
    pallas_call x1, Pallas kernels, local(): pl.pallas_call(functools.partial(panel_kernel, order, 512), out_shape=(sh...  12 us
    unnamed x6, local copies, waits for them, and re-layouts  7.55 us

profile of v1, /device:TPU:1, one launch (start us, length us, event | category | flops | bytes accessed | tf_op | source)
XLA Modules:
  0.0 36.2 jit_solution(12747450899022738001)
XLA Ops:
  0.6 12.0 %panels.1 = (f32[1024,128]{1,0:T(8,128)}, f32[64,128]{1,0:T(8,128)}, f32[16,128]{1,0:T(8,128)}, f32[8,128]{1,0:T(8,128)}) custom-call(f32[2,1,1,8192]{3,2,1,0:T(1,128)} %off_ref.1, f32[2,1,1,8192]{3,2,1,0:T(1,128)} %str_ref.1, s32[1,1,8192]{2,1,0:T(1,128)} %map_ref.1, f32[7,4,128,128]{3,2,1,0:T(8,128)} %shift_ref.3), custom_call_target="tpu_custom_call" | custom-call | tf_op jit(solution)/shard_map/panels/pallas_call | solution.py:368
  12.6 16.0 %exchange.1 = (f32[1,1,128]{2,1,0:T(1,128)}, f32[2,2,128]{2,1,0:T(2,128)}, f32[4,4,128]{2,1,0:T(4,128)}, f32[8,8,128]{2,1,0:T(8,128)}, f32[4,2,128]{2,1,0:T(2,128)}, /*index=5*/f32[2,1,128]{2,1,0:T(1,128)}) custom-call(f32[8,8,128]{2,1,0:T(8,128)} %bitcast.2, f32[16,128]{1,0:T(8,128)} %get-tuple-element.19.l2_ref, f32[8,128]{1,0:T(8,128)} %get-tuple-element.20.l01_ref, ...), custom_call_target="tpu_custom_call" | custom-call | tf_op jit(solution)/shard_map/exchange/pallas_call | solution.py:378
  28.6 1.1 %copy.18 = f32[1,1,128]{2,1,0:T(1,128)} copy(f32[1,1,128]{2,1,0:T(1,128)} %get-tuple-element.35) | data formatting | bytes 1024
  29.7 1.3 %copy.19 = f32[2,2,128]{2,1,0:T(2,128)} copy(f32[2,2,128]{2,1,0:T(2,128)} %get-tuple-element.36) | data formatting | bytes 4096
  31.0 1.3 %copy.20 = f32[4,4,128]{2,1,0:T(4,128)} copy(f32[4,4,128]{2,1,0:T(4,128)} %get-tuple-element.37) | data formatting | bytes 16384
  32.3 1.4 %copy.21 = f32[8,8,128]{2,1,0:T(8,128)} copy(f32[8,8,128]{2,1,0:T(8,128)} %get-tuple-element.38) | data formatting | bytes 65536
  33.7 1.3 %copy.22 = f32[4,2,128]{2,1,0:T(2,128)} copy(f32[4,2,128]{2,1,0:T(2,128)} %get-tuple-element.39) | data formatting | bytes 8192
  34.9 1.2 %copy.23 = f32[2,1,128]{2,1,0:T(1,128)} copy(f32[2,1,128]{2,1,0:T(1,128)} %get-tuple-element.40) | data formatting | bytes 2048

commit v2 on v1

--- a/solution.py
+++ b/solution.py
@@ -1,4 +1,5 @@
 import functools
+import math
 
 import jax
 import jax.numpy as jnp
@@ -12,6 +13,7 @@
 MESH = pl.DeviceIdType.MESH
 COARSE = 2
 SIDE = 32
+CHUNK = 2048
 REACH = 3
 
 
@@ -46,9 +48,8 @@
     return t[8] + t[8], prev, cur
 
 
-def panel_kernel(order, chunk, off_ref, str_ref, map_ref, shift_ref, leaf_ref, l3_ref, l2_ref, l01_ref, acc_ref):
+def panel_sums(order, chunk, off_ref, str_ref, map_ref, leaf_ref, acc_ref):
     panels = off_ref.shape[-1]
-    leaves = SIDE * SIDE
     acc_ref[...] = jnp.zeros_like(acc_ref)
 
     def body(i, carry):
@@ -80,6 +81,10 @@
     width = 2 * order
     leaf_ref[...] = acc_ref[:, :width] + acc_ref[:, width:]
 
+
+def upward(shift_ref, leaf_ref, l3_ref, l2_ref):
+    width = leaf_ref.shape[-1]
+
     def weight(level):
         return shift_ref[COARSE + level].reshape(4 * width, width)
 
@@ -107,7 +112,7 @@
             parts.append(jnp.concatenate([l2_ref[pl.ds((2 * r + rb) * 4 + cb, 2, stride=2), :] for r in range(2)], axis=0))
     level1 = merge(parts, weight(1))
     level0 = merge([level1[q : q + 1] for q in range(4)], weight(0))
-    l01_ref[...] = jnp.concatenate([level0, level1, jnp.zeros((3, width), F32)], axis=0)
+    return jnp.concatenate([level0, level1, jnp.zeros((3, width), F32)], axis=0)
 
 
 NEAR = [(dr, dc) for dr in range(-3, 4) for dc in range(-3, 4) if max(abs(dr), abs(dc)) >= 2]
@@ -118,27 +123,44 @@
     return -2 - parity <= d <= 3 - parity
 
 
-def exchange_kernel(
-    rows, cols,
-    l3_ref, l2_ref, l01_ref, shift_ref, diag_ref,
-    zero_out, one_out, two_out, three_out, coarse_out, top_out,
-    reg3, slots2, big, pad2, sh3, sh2, xr, xi, lhs, grid1,
+def tree_kernel(
+    rows, cols, chunk,
+    off_ref, str_ref, map_ref, shift_in, diag_in,
+    leaf_ref, zero_out, one_out, two_out, three_out, coarse_out, top_out,
+    acc_ref, shift_ref, diag_ref, l3_flat, l3_ref, l2_ref, l01_ref, load_sem, reg3, slots2, big, pad2, sh3, sh2, xr, xi, lhs, grid1,
     send_all, recv_all, send_near, recv_near,
 ):
     w, v = lax.axis_index("wide"), lax.axis_index("narrow")
     count = rows * cols
-    me = w * cols + v
-    width = l01_ref.shape[-1]
+    width = diag_ref.shape[-1]
     half = width // 2
 
+    to_w = [lax.rem(w + i, rows) for i in range(rows)]
+    to_v = [lax.rem(v + j, cols) for j in range(cols)]
+    from_w = [lax.rem(w + rows - i, rows) for i in range(rows)]
+    from_v = [lax.rem(v + cols - j, cols) for j in range(cols)]
+    others = [(i, j) for i in range(rows) for j in range(cols) if (i, j) != (0, 0)]
+
     barrier = pltpu.get_barrier_semaphore()
-
-    def greet(i, carry):
-        t = lax.rem(me + i, count)
-        pl.semaphore_signal(barrier, inc=1, device_id=(t // cols, lax.rem(t, cols)), device_id_type=MESH)
-        return carry
-
-    lax.fori_loop(1, count, greet, 0)
+    for i, j in others:
+        pl.semaphore_signal(barrier, inc=1, device_id=(to_w[i], to_v[j]), device_id_type=MESH)
+    loads = [
+        pltpu.make_async_copy(shift_in, shift_ref, load_sem.at[0]),
+        pltpu.make_async_copy(diag_in, diag_ref, load_sem.at[1]),
+    ]
+    for load in loads:
+        load.start()
+
+    panel_sums(half, chunk, off_ref, str_ref, map_ref, leaf_ref, acc_ref)
+    for load in loads:
+        load.wait()
+    l01_ref[...] = upward(shift_ref, leaf_ref, l3_flat, l2_ref)
+    for r in range(8):
+        block = l3_flat[pl.ds(8 * r, 8)]
+        l3_ref[r] = block
+        reg3[3 + r, pl.ds(8, 8)] = block
+    slots2[4] = l2_ref[...]
+    big[3 + w, 3 + v] = l01_ref[...]
     pl.semaphore_wait(barrier, count - 1)
 
     row_of = {-1: 0, 0: 0, 1: 5}
@@ -172,18 +194,14 @@
             device_id=target, device_id_type=MESH)
         return three, two
 
-    def all_copy(t, source):
-        sw, sv = source // cols, lax.rem(source, cols)
+    def all_copy(i, j, source):
         return pltpu.make_async_remote_copy(
-            src_ref=l01_ref, dst_ref=big.at[3 + sw, 3 + sv],
-            send_sem=send_all.at[t], recv_sem=recv_all.at[source],
-            device_id=(t // cols, lax.rem(t, cols)), device_id_type=MESH)
-
-    def send(i, carry):
-        all_copy(lax.rem(me + i, count), me).start()
-        return carry
-
-    lax.fori_loop(1, count, send, 0)
+            src_ref=l01_ref, dst_ref=big.at[3 + source[0], 3 + source[1]],
+            send_sem=send_all.at[i * cols + j], recv_sem=recv_all.at[i * cols + j],
+            device_id=(to_w[i], to_v[j]), device_id_type=MESH)
+
+    for i, j in others:
+        all_copy(i, j, (w, v)).start()
     for dw, dv in AROUND:
         @pl.when(inside(dw, dv))
         def _():
@@ -202,10 +220,6 @@
         for c in range(cols + 6):
             if not (3 <= r < rows + 3 and 3 <= c < cols + 3):
                 big[r, c] = tile
-    big[3 + w, 3 + v] = l01_ref[...]
-    for r in range(8):
-        reg3[3 + r, pl.ds(8, 8)] = l3_ref[r]
-    slots2[4] = l2_ref[...]
     for r in range(10):
         pad2[r, pl.ds(8, 8)] = tile
 
@@ -269,12 +283,8 @@
             sh2[dc + 3, r] = col_mask(dc, pad2[r, pl.ds(4 + dc, 8)])
     near_level(3, 4, sh2, two_out)
 
-    def arrive(i, carry):
-        s = lax.rem(me + i, count)
-        all_copy(s, s).wait_recv()
-        return carry
-
-    lax.fori_loop(1, count, arrive, 0)
+    for i, j in others:
+        all_copy(i, j, (from_w[i], from_v[j])).wait_recv()
 
     half_r, half_c = rows // 2, cols // 2
     for r in range(rows):
@@ -351,40 +361,45 @@
             for copy in near_copies(dw, dv):
                 copy.wait_send()
 
-    def left(i, carry):
-        all_copy(lax.rem(me + i, count), me).wait_send()
-        return carry
-
-    lax.fori_loop(1, count, left, 0)
+    for i, j in others:
+        all_copy(i, j, (w, v)).wait_send()
+
+
+def write_kernel(n, *refs):
+    sem = refs[2 * n]
+    copies = [pltpu.make_async_copy(refs[k], refs[n + k], sem.at[k]) for k in range(n)]
+    for copy in copies:
+        copy.start()
+    for copy in copies:
+        copy.wait()
 
 
 def local(mesh_shape, offsets, strengths, leaf_map, shift_matrices, transfer_diagonal):
     rows, cols = mesh_shape
     width = shift_matrices.shape[-1]
-    order = width // 2
     levels = transfer_diagonal.shape[0]
     vmem = pl.BlockSpec(memory_space=pltpu.VMEM)
-    shape = lambda *dims: jax.ShapeDtypeStruct(dims, F32)
-    leaf, l3, l2, l01 = pl.pallas_call(
-        functools.partial(panel_kernel, order, 512),
-        out_shape=(shape(SIDE * SIDE, width), shape(64, width), shape(16, width), shape(8, width)),
-        in_specs=[vmem] * 4,
-        out_specs=(vmem,) * 4,
-        scratch_shapes=[pltpu.VMEM((SIDE * SIDE, 2 * width), F32)],
-        name="panels",
-    )(offsets, strengths, leaf_map, shift_matrices)
     boxes = (rows // 2) * (cols // 2)
     pad8 = -(-boxes // 8) * 8
-    outs = pl.pallas_call(
-        functools.partial(exchange_kernel, rows, cols),
-        out_shape=(
-            shape(1, 1, width), shape(2, 2, width), shape(4, 4, width), shape(8, 8, width),
-            shape(rows // 2, cols // 2, width), shape(rows // 4, cols // 4, width),
-        ),
-        grid=(1,),
-        in_specs=[vmem, vmem, vmem, pl.BlockSpec((2, 4, width, width), lambda i: (0, 0, 0, 0)), vmem],
-        out_specs=(vmem,) * 6,
+    dims = (
+        (SIDE * SIDE, width), (1, 1, width), (2, 2, width), (4, 4, width), (8, 8, width),
+        (rows // 2, cols // 2, width), (rows // 4, cols // 4, width),
+    )
+    any_space = pl.BlockSpec(memory_space=pl.ANY)
+    held = pl.pallas_call(
+        functools.partial(tree_kernel, rows, cols, math.gcd(CHUNK, offsets.shape[-1])),
+        out_shape=tuple(pltpu.VMEM(d, F32) for d in dims),
+        in_specs=[vmem, vmem, vmem, any_space, any_space],
+        out_specs=(vmem,) * len(dims),
         scratch_shapes=[
+            pltpu.VMEM((SIDE * SIDE, 2 * width), F32),
+            pltpu.VMEM(shift_matrices.shape, F32),
+            pltpu.VMEM(transfer_diagonal.shape, F32),
+            pltpu.VMEM((64, width), F32),
+            pltpu.VMEM((8, 8, width), F32),
+            pltpu.VMEM((16, width), F32),
+            pltpu.VMEM((8, width), F32),
+            pltpu.SemaphoreType.DMA((2,)),
             pltpu.VMEM((14, 24, width), F32),
             pltpu.VMEM((9, 16, width), F32),
             pltpu.VMEM((rows + 6, cols + 6, 8, width), F32),
@@ -401,9 +416,18 @@
             pltpu.SemaphoreType.DMA((2, 9)),
         ],
         compiler_params=pltpu.CompilerParams(collective_id=0, has_side_effects=True),
-        name="exchange",
-    )(l3.reshape(8, 8, width), l2, l01, shift_matrices, transfer_diagonal)
-    return (leaf.reshape(SIDE, SIDE, width),) + tuple(outs)
+        name="tree",
+    )(offsets, strengths, leaf_map, shift_matrices, transfer_diagonal)
+    n = len(dims)
+    outs = pl.pallas_call(
+        functools.partial(write_kernel, n),
+        out_shape=tuple(jax.ShapeDtypeStruct(d, F32) for d in dims),
+        in_specs=[vmem] * n,
+        out_specs=(any_space,) * n,
+        scratch_shapes=[pltpu.SemaphoreType.DMA((n,))],
+        name="write",
+    )(*[pltpu.with_memory_space_constraint(x, pltpu.VMEM) for x in held])
+    return (outs[0].reshape(SIDE, SIDE, width),) + tuple(outs[1:])
 
 
 def solution(mesh):

time: 36.5 us -> 19.7 us (0.54)
  the two profiles are of different devices: /device:TPU:1 before, /device:TPU:0 now
where the time goes in v2:
time: 19.7 us; the launch traced here: 19.5 us
  Pallas kernels  18.9 us (96%)
  between operations  0.64 us (3%)
    pallas_call x1, Pallas kernels, local(): pl.pallas_call(functools.partial(tree_kernel, rows, cols, math.gcd(CHUNK,...  18 us
    pallas_call x1, Pallas kernels, local(): pl.pallas_call(functools.partial(write_kernel, n), out_shape=tuple((jax.S...  0.87 us

profile of v2, /device:TPU:0, one launch (start us, length us, event | category | flops | bytes accessed | tf_op | source)
XLA Modules:
  0.0 19.5 jit_solution(13185446960390107601)
XLA Ops:
  0.6 18.0 %tree.1 = (f32[1024,128]{1,0:T(8,128)S(1)}, f32[1,1,128]{2,1,0:T(1,128)S(1)}, f32[2,2,128]{2,1,0:T(2,128)S(1)}, f32[4,4,128]{2,1,0:T(4,128)S(1)}, f32[8,8,128]{2...) custom-call(f32[2,1,1,8192]{3,2,1,0:T(1,128)} %off_ref.1, f32[2,1,1,8192]{3,2,1,0:T(1,128)} %str_ref.1, ...), custom_call_target="tpu_custom_call" | custom-call | tf_op jit(solution)/shard_map/tree/pallas_call | solution.py:389
  18.6 0.9 %write.1 = (f32[1024,128]{1,0:T(8,128)}, f32[1,1,128]{2,1,0:T(1,128)}, f32[2,2,128]{2,1,0:T(2,128)}, f32[4,4,128]{2,1,0:T(4,128)}, f32[8,8,128]{2,1,0:T(8,128)},...) custom-call(f32[1024,128]{1,0:T(8,128)S(1)} %get-tuple-element.21.refs_0_, f32[1,1,128]{2,1,0:T(1,128)S(1)} %get-tuple-element.22.refs_1_, ...), custom_call_target="tpu_custom_call" | custom-call | tf_op jit(solution)/shard_map/write/pallas_call | solution.py:422

commit v3 on v2

--- a/solution.py
+++ b/solution.py
@@ -14,7 +14,6 @@
 COARSE = 2
 SIDE = 32
 CHUNK = 2048
-REACH = 3
 
 
 def split(x):
@@ -24,15 +23,18 @@
 
 def dot(a, b):
     return jnp.dot(a, b, preferred_element_type=F32)
+
+
+def halves(weight):
+    return jnp.concatenate(split(weight), axis=1)
 
 
 def merge(parts, weight):
     width = parts[0].shape[1]
     lhs = jnp.concatenate(parts, axis=1)
     hi, lo = split(lhs)
-    w_hi, w_lo = split(weight)
-    both = dot(hi, jnp.concatenate([w_hi, w_lo], axis=1))
-    return both[:, :width] + (both[:, width:] + dot(lo, w_hi))
+    both = dot(hi, weight)
+    return both[:, :width] + (both[:, width:] + dot(lo, weight[:, :width]))
 
 
 def cheb_start(a):
@@ -50,9 +52,8 @@
 
 def panel_sums(order, chunk, off_ref, str_ref, map_ref, leaf_ref, acc_ref):
     panels = off_ref.shape[-1]
-    acc_ref[...] = jnp.zeros_like(acc_ref)
-
-    def body(i, carry):
+
+    def add(i, first):
         at = pl.ds(pl.multiple_of(i * chunk, chunk), chunk)
         wide8 = lambda ref, n: jnp.broadcast_to(ref[n, 0, :, at], (8, chunk))
         a, b = wide8(off_ref, 0), wide8(off_ref, 1)
@@ -74,10 +75,15 @@
         one = (col == lax.broadcasted_iota(jnp.int32, (SIDE, chunk), 0)).astype(F32).astype(BF16)
         zero = jnp.zeros_like(one)
         sel = jnp.concatenate([jnp.where(row == r, one, zero) for r in range(SIDE)], axis=0)
-        acc_ref[...] += lax.dot_general(sel, terms, (((1,), (1,)), ((), ())), preferred_element_type=F32)
+        part = lax.dot_general(sel, terms, (((1,), (1,)), ((), ())), preferred_element_type=F32)
+        acc_ref[...] = part if first else acc_ref[...] + part
+
+    def body(i, carry):
+        add(i, False)
         return carry
 
-    lax.fori_loop(0, panels // chunk, body, 0)
+    add(0, True)
+    lax.fori_loop(1, panels // chunk, body, 0)
     width = 2 * order
     leaf_ref[...] = acc_ref[:, :width] + acc_ref[:, width:]
 
@@ -86,7 +92,7 @@
     width = leaf_ref.shape[-1]
 
     def weight(level):
-        return shift_ref[COARSE + level].reshape(4 * width, width)
+        return halves(shift_ref[COARSE + level].reshape(4 * width, width))
 
     parts = []
     for r0 in range(2):
@@ -112,7 +118,7 @@
             parts.append(jnp.concatenate([l2_ref[pl.ds((2 * r + rb) * 4 + cb, 2, stride=2), :] for r in range(2)], axis=0))
     level1 = merge(parts, weight(1))
     level0 = merge([level1[q : q + 1] for q in range(4)], weight(0))
-    return jnp.concatenate([level0, level1, jnp.zeros((3, width), F32)], axis=0)
+    return level1, level0
 
 
 NEAR = [(dr, dc) for dr in range(-3, 4) for dc in range(-3, 4) if max(abs(dr), abs(dc)) >= 2]
@@ -127,7 +133,8 @@
     rows, cols, chunk,
     off_ref, str_ref, map_ref, shift_in, diag_in,
     leaf_ref, zero_out, one_out, two_out, three_out, coarse_out, top_out,
-    acc_ref, shift_ref, diag_ref, l3_flat, l3_ref, l2_ref, l01_ref, load_sem, reg3, slots2, big, pad2, sh3, sh2, xr, xi, lhs, grid1,
+    acc_ref, shift_ref, diag_ref, l3_ref, l2_ref, l1_ref, l0_ref, load_sem,
+    packed, landed, big, win3, win2, win1, sh3, sh2, sh1, xr, xi, lhs, grid1, coarse_w,
     send_all, recv_all, send_near, recv_near,
 ):
     w, v = lax.axis_index("wide"), lax.axis_index("narrow")
@@ -154,19 +161,27 @@
     panel_sums(half, chunk, off_ref, str_ref, map_ref, leaf_ref, acc_ref)
     for load in loads:
         load.wait()
-    l01_ref[...] = upward(shift_ref, leaf_ref, l3_flat, l2_ref)
-    for r in range(8):
-        block = l3_flat[pl.ds(8 * r, 8)]
-        l3_ref[r] = block
-        reg3[3 + r, pl.ds(8, 8)] = block
-    slots2[4] = l2_ref[...]
-    big[3 + w, 3 + v] = l01_ref[...]
+    level1, level0 = upward(shift_ref, leaf_ref, l3_ref, l2_ref)
+    l0_ref[...] = level0
+    l1_ref[...] = jnp.concatenate([level1, jnp.zeros((4, width), F32)], axis=0)
+
+    edge = {-1: 0, 1: 1}
+    for dw, dv in AROUND:
+        at = (1 + dw) * 3 + 1 + dv
+        one_at = 24 if 0 in (dw, dv) else 8
+        packed[at, pl.ds(one_at, 8)] = l1_ref[...]
+        if dv == 0:
+            packed[at, pl.ds(0, 16)] = l3_ref[pl.ds(48 * edge[dw], 16)]
+            packed[at, pl.ds(16, 8)] = l2_ref[pl.ds(8 * edge[dw], 8)]
+        elif dw == 0:
+            for k in range(2):
+                packed[at, pl.ds(8 * k, 8)] = l3_ref[pl.ds(6 * edge[dv] + k, 8, stride=8)]
+                packed[at, pl.ds(16 + 4 * k, 4)] = l2_ref[pl.ds(2 * edge[dv] + k, 4, stride=4)]
+        else:
+            for k in range(2):
+                packed[at, pl.ds(2 * k, 2)] = l3_ref[pl.ds((6 * edge[dw] + k) * 8 + 6 * edge[dv], 2)]
+                packed[at, pl.ds(4 + 2 * k, 2)] = l2_ref[pl.ds((2 * edge[dw] + k) * 4 + 2 * edge[dv], 2)]
     pl.semaphore_wait(barrier, count - 1)
-
-    row_of = {-1: 0, 0: 0, 1: 5}
-    row_to = {-1: 11, 0: 3, 1: 0}
-    row_n = {-1: 3, 0: 8, 1: 3}
-    col_to = {-1: 16, 0: 8, 1: 0}
 
     def inside(dw, dv):
         ok = jnp.bool_(True)
@@ -180,23 +195,17 @@
             ok = ok & (v < cols - 1)
         return ok
 
-    def near_copies(dw, dv):
-        slot = (1 - dw) * 3 + (1 - dv)
-        target = (w + dw, v + dv)
-        three = pltpu.make_async_remote_copy(
-            src_ref=l3_ref.at[pl.ds(row_of[dw], row_n[dw])],
-            dst_ref=reg3.at[pl.ds(row_to[dw], row_n[dw]), pl.ds(col_to[dv], 8)],
-            send_sem=send_near.at[0, slot], recv_sem=recv_near.at[0, slot],
-            device_id=target, device_id_type=MESH)
-        two = pltpu.make_async_remote_copy(
-            src_ref=l2_ref, dst_ref=slots2.at[slot],
-            send_sem=send_near.at[1, slot], recv_sem=recv_near.at[1, slot],
-            device_id=target, device_id_type=MESH)
-        return three, two
+    def near_copy(dw, dv):
+        out_at, in_at = (1 + dw) * 3 + 1 + dv, (1 - dw) * 3 + 1 - dv
+        n = 32 if 0 in (dw, dv) else 16
+        return pltpu.make_async_remote_copy(
+            src_ref=packed.at[out_at, pl.ds(0, n)], dst_ref=landed.at[in_at, pl.ds(0, n)],
+            send_sem=send_near.at[in_at], recv_sem=recv_near.at[in_at],
+            device_id=(w + dw, v + dv), device_id_type=MESH)
 
     def all_copy(i, j, source):
         return pltpu.make_async_remote_copy(
-            src_ref=l01_ref, dst_ref=big.at[3 + source[0], 3 + source[1]],
+            src_ref=l0_ref, dst_ref=big.at[3 + source[0], 3 + source[1]],
             send_sem=send_all.at[i * cols + j], recv_sem=recv_all.at[i * cols + j],
             device_id=(to_w[i], to_v[j]), device_id_type=MESH)
 
@@ -205,23 +214,17 @@
     for dw, dv in AROUND:
         @pl.when(inside(dw, dv))
         def _():
-            for copy in near_copies(dw, dv):
-                copy.start()
-
-    tile = jnp.zeros((8, width), F32)
+            near_copy(dw, dv).start()
+
     for dw, dv in AROUND:
         @pl.when(jnp.logical_not(inside(dw, dv)))
         def _():
-            for r in range(row_n[-dw]):
-                reg3[row_to[-dw] + r, pl.ds(col_to[-dv], 8)] = tile
-            slot = (1 + dw) * 3 + (1 + dv)
-            slots2[slot] = jnp.zeros((16, width), F32)
+            landed[(1 + dw) * 3 + 1 + dv] = jnp.zeros((32, width), F32)
     for r in range(rows + 6):
         for c in range(cols + 6):
             if not (3 <= r < rows + 3 and 3 <= c < cols + 3):
-                big[r, c] = tile
-    for r in range(10):
-        pad2[r, pl.ds(8, 8)] = tile
+                big[r, c] = jnp.zeros((1, width), F32)
+    big[3 + w, 3 + v] = l0_ref[...]
 
     lane = lax.broadcasted_iota(jnp.int32, (diag_ref.shape[1], width), 1) < half
     for s in range(diag_ref.shape[0]):
@@ -229,9 +232,10 @@
         turned = pltpu.roll(d, half, 1)
         xr[s] = jnp.where(lane, d, turned)
         xi[s] = jnp.where(lane, turned, d)
+    for t in range(COARSE):
+        coarse_w[t] = halves(shift_ref[t].reshape(4 * width, width))
     sign = jnp.where(lax.broadcasted_iota(jnp.int32, (1, width), 1) < half, -1.0, 1.0).astype(F32)
-    c_id = lax.broadcasted_iota(jnp.int32, (8, width), 0)
-    odd = lax.rem(c_id, 2) == 1
+    odd = lax.rem(lax.broadcasted_iota(jnp.int32, (8, width), 0), 2) == 1
 
     def col_mask(dc, slab):
         if dc == -3:
@@ -247,14 +251,25 @@
     def finish(acc_r, acc_i):
         return acc_r + sign * pltpu.roll(acc_i, half, 1)
 
-    def near_level(s, n, shifted, out):
+    for r in range(8):
+        win3[pl.ds((2 + r) * 24 + 8, 8)] = l3_ref[pl.ds(8 * r, 8)]
+    for r in range(4):
+        win2[pl.ds((2 + r) * 16 + 4, 4)] = l2_ref[pl.ds(4 * r, 4)]
+    for r in range(2):
+        win1[pl.ds((2 + r) * 16 + 4, 2)] = l1_ref[pl.ds(2 * r, 2)]
+
+    def near_level(s, n, window, pitch, shifted, out):
+        left = 8 if n == 8 else 4
+        for dc in range(-3, 4):
+            for r in range(n + 4):
+                shifted[dc + 3, r] = col_mask(dc, window[pl.ds(r * pitch + left + dc, 8)])
         acc_r = [jnp.zeros((8, width), F32) for _ in range(n)]
         acc_i = [jnp.zeros((8, width), F32) for _ in range(n)]
         for dr, dc in NEAR:
             f_r, f_i = factor(s, dr, dc)
             for r in range(n):
                 if allowed(dr, r % 2):
-                    src = shifted[dc + 3, 3 + r + dr]
+                    src = shifted[dc + 3, 2 + r + dr]
                     acc_r[r] = acc_r[r] + f_r * src
                     acc_i[r] = acc_i[r] + f_i * src
         for r in range(n):
@@ -263,25 +278,29 @@
     for dw, dv in AROUND:
         @pl.when(inside(dw, dv))
         def _():
-            for copy in near_copies(-dw, -dv):
-                copy.wait_recv()
-
-    for dc in range(-3, 4):
-        for r in range(14):
-            sh3[dc + 3, r] = col_mask(dc, reg3[r, pl.ds(8 + dc, 8)])
-    near_level(4, 8, sh3, three_out)
-
-    for dw in (-1, 0, 1):
-        for dv in (-1, 0, 1):
-            slot = (1 + dw) * 3 + (1 + dv)
-            for r in range(4):
-                at = 3 + 4 * dw + r
-                if 0 <= at < 10:
-                    pad2[at, pl.ds(4 + 4 * dv, 4)] = slots2[slot, pl.ds(4 * r, 4)]
-    for dc in range(-3, 4):
-        for r in range(10):
-            sh2[dc + 3, r] = col_mask(dc, pad2[r, pl.ds(4 + dc, 8)])
-    near_level(3, 4, sh2, two_out)
+            near_copy(-dw, -dv).wait_recv()
+
+    for dw, dv in AROUND:
+        at = (1 + dw) * 3 + 1 + dv
+        first = lambda d, n: {-1: 0, 0: 2, 1: n + 2}[d]
+        column = lambda d, n, left: {-1: left - 2, 0: left, 1: left + n}[d]
+        r3, r2, r1 = first(dw, 8), first(dw, 4), first(dw, 2)
+        c3, c2, c1 = column(dv, 8, 8), column(dv, 4, 4), column(dv, 2, 4)
+        one_at = 24 if 0 in (dw, dv) else 8
+        for k in range(2):
+            win1[pl.ds((r1 + k) * 16 + c1, 2)] = landed[at, pl.ds(one_at + 2 * k, 2)]
+            if dv == 0:
+                win3[pl.ds((r3 + k) * 24 + c3, 8)] = landed[at, pl.ds(8 * k, 8)]
+                win2[pl.ds((r2 + k) * 16 + c2, 4)] = landed[at, pl.ds(16 + 4 * k, 4)]
+            elif dw == 0:
+                win3[pl.ds(r3 * 24 + c3 + k, 8, stride=24)] = landed[at, pl.ds(8 * k, 8)]
+                win2[pl.ds(r2 * 16 + c2 + k, 4, stride=16)] = landed[at, pl.ds(16 + 4 * k, 4)]
+            else:
+                win3[pl.ds((r3 + k) * 24 + c3, 2)] = landed[at, pl.ds(2 * k, 2)]
+                win2[pl.ds((r2 + k) * 16 + c2, 2)] = landed[at, pl.ds(4 + 2 * k, 2)]
+    near_level(4, 8, win3, 24, sh3, three_out)
+    near_level(3, 4, win2, 16, sh2, two_out)
+    near_level(2, 2, win1, 16, sh1, one_out)
 
     for i, j in others:
         all_copy(i, j, (from_w[i], from_v[j])).wait_recv()
@@ -290,13 +309,10 @@
     for r in range(rows):
         for c in range(cols):
             q = 2 * (r % 2) + c % 2
-            lhs[pl.ds((r // 2) * half_c + c // 2, 1), pl.ds(q * width, width)] = big[3 + r, 3 + c, pl.ds(0, 1)]
+            lhs[pl.ds((r // 2) * half_c + c // 2, 1), pl.ds(q * width, width)] = big[3 + r, 3 + c]
     boxes = half_r * half_c
 
-    def weight(t):
-        return shift_ref[t].reshape(4 * width, width)
-
-    coarse = merge([lhs[:boxes, pl.ds(q * width, width)] for q in range(4)], weight(1))
+    coarse = merge([lhs[:boxes, pl.ds(q * width, width)] for q in range(4)], coarse_w[1])
     grid1[:boxes] = coarse
     quarter_c = half_c // 2
     for r in range(half_r):
@@ -304,24 +320,9 @@
             q = 2 * (r % 2) + c % 2
             lhs[pl.ds((r // 2) * quarter_c + c // 2, 1), pl.ds(q * width, width)] = grid1[pl.ds(r * half_c + c, 1)]
     tops = (half_r // 2) * quarter_c
-    top = merge([lhs[:tops, pl.ds(q * width, width)] for q in range(4)], weight(0))
+    top = merge([lhs[:tops, pl.ds(q * width, width)] for q in range(4)], coarse_w[0])
     for r in range(half_r // 2):
         top_out[r] = top[r * quarter_c : (r + 1) * quarter_c]
-
-    for tr in range(2):
-        line = []
-        for tc in range(2):
-            acc_r = jnp.zeros((1, width), F32)
-            acc_i = jnp.zeros((1, width), F32)
-            for dr, dc in NEAR:
-                if allowed(dr, tr) and allowed(dc, tc):
-                    f_r, f_i = factor(2, dr, dc)
-                    sr, sc = tr + dr, tc + dc
-                    src = big[3 + w + sr // 2, 3 + v + sc // 2, pl.ds(1 + 2 * (sr % 2) + sc % 2, 1)]
-                    acc_r = acc_r + f_r * src
-                    acc_i = acc_i + f_i * src
-            line.append(finish(acc_r, acc_i))
-        one_out[tr] = jnp.concatenate(line, axis=0)
 
     odd_w, odd_v = lax.rem(w, 2), lax.rem(v, 2)
     keep = {
@@ -332,7 +333,7 @@
     acc_i = jnp.zeros((1, width), F32)
     for dr, dc in NEAR:
         f_r, f_i = factor(1, dr, dc)
-        src = big[3 + w + dr, 3 + v + dc, pl.ds(0, 1)]
+        src = big[3 + w + dr, 3 + v + dc]
         if abs(dr) == 3:
             src = src * keep["r", dr]
         if abs(dc) == 3:
@@ -358,8 +359,7 @@
     for dw, dv in AROUND:
         @pl.when(inside(dw, dv))
         def _():
-            for copy in near_copies(dw, dv):
-                copy.wait_send()
+            near_copy(dw, dv).wait_send()
 
     for i, j in others:
         all_copy(i, j, (w, v)).wait_send()
@@ -396,24 +396,28 @@
             pltpu.VMEM(shift_matrices.shape, F32),
             pltpu.VMEM(transfer_diagonal.shape, F32),
             pltpu.VMEM((64, width), F32),
-            pltpu.VMEM((8, 8, width), F32),
             pltpu.VMEM((16, width), F32),
             pltpu.VMEM((8, width), F32),
+            pltpu.VMEM((1, width), F32),
             pltpu.SemaphoreType.DMA((2,)),
-            pltpu.VMEM((14, 24, width), F32),
-            pltpu.VMEM((9, 16, width), F32),
-            pltpu.VMEM((rows + 6, cols + 6, 8, width), F32),
-            pltpu.VMEM((10, 16, width), F32),
-            pltpu.VMEM((7, 14, 8, width), F32),
-            pltpu.VMEM((7, 10, 8, width), F32),
+            pltpu.VMEM((9, 32, width), F32),
+            pltpu.VMEM((9, 32, width), F32),
+            pltpu.VMEM((rows + 6, cols + 6, 1, width), F32),
+            pltpu.VMEM((12 * 24, width), F32),
+            pltpu.VMEM((8 * 16, width), F32),
+            pltpu.VMEM((6 * 16, width), F32),
+            pltpu.VMEM((7, 12, 8, width), F32),
+            pltpu.VMEM((7, 8, 8, width), F32),
+            pltpu.VMEM((7, 6, 8, width), F32),
             pltpu.VMEM((levels, 49, width), F32),
             pltpu.VMEM((levels, 49, width), F32),
             pltpu.VMEM((pad8, 4 * width), F32),
             pltpu.VMEM((pad8, width), F32),
+            pltpu.VMEM((COARSE, 4 * width, 2 * width), BF16),
             pltpu.SemaphoreType.DMA((rows * cols,)),
             pltpu.SemaphoreType.DMA((rows * cols,)),
-            pltpu.SemaphoreType.DMA((2, 9)),
-            pltpu.SemaphoreType.DMA((2, 9)),
+            pltpu.SemaphoreType.DMA((9,)),
+            pltpu.SemaphoreType.DMA((9,)),
         ],
         compiler_params=pltpu.CompilerParams(collective_id=0, has_side_effects=True),
         name="tree",

time: 19.7 us -> 19.2 us (0.975)
  Pallas kernels: 18.9 us -> 18.4 us
    pallas_call x1, Pallas kernels: 18 us -> 17.6 us  [local(): pl.pallas_call(functools.partial(tree_kernel, rows, cols, math.gcd(CHUNK,...]
where the time goes in v3:
time: 19.2 us; the launch traced here: 19.1 us
  Pallas kernels  18.4 us (96%)
  between operations  0.64 us (3%)
    pallas_call x1, Pallas kernels, local(): pl.pallas_call(functools.partial(tree_kernel, rows, cols, math.gcd(CHUNK,...  17.6 us
    pallas_call x1, Pallas kernels, local(): pl.pallas_call(functools.partial(write_kernel, n), out_shape=tuple((jax.S...  0.87 us

profile of v3, /device:TPU:0, one launch (start us, length us, event | category | flops | bytes accessed | tf_op | source)
XLA Modules:
  0.0 19.1 jit_solution(6302111855841181470)
XLA Ops:
  0.6 17.6 %tree.1 = (f32[1024,128]{1,0:T(8,128)S(1)}, f32[1,1,128]{2,1,0:T(1,128)S(1)}, f32[2,2,128]{2,1,0:T(2,128)S(1)}, f32[4,4,128]{2,1,0:T(4,128)S(1)}, f32[8,8,128]{2...) custom-call(f32[2,1,1,8192]{3,2,1,0:T(1,128)} %off_ref.1, f32[2,1,1,8192]{3,2,1,0:T(1,128)} %str_ref.1, ...), custom_call_target="tpu_custom_call" | custom-call | tf_op jit(solution)/shard_map/tree/pallas_call | solution.py:389
  18.2 0.9 %write.1 = (f32[1024,128]{1,0:T(8,128)}, f32[1,1,128]{2,1,0:T(1,128)}, f32[2,2,128]{2,1,0:T(2,128)}, f32[4,4,128]{2,1,0:T(4,128)}, f32[8,8,128]{2,1,0:T(8,128)},...) custom-call(f32[1024,128]{1,0:T(8,128)S(1)} %get-tuple-element.21.refs_0_, f32[1,1,128]{2,1,0:T(1,128)S(1)} %get-tuple-element.22.refs_1_, ...), custom_call_target="tpu_custom_call" | custom-call | tf_op jit(solution)/shard_map/write/pallas_call | solution.py:426
